TPU v7x, 32 devices: a whole 2x2x4 slice. The times are simulated.
32 devices in a mesh: parts: 2 (over x), blk: 16 (over z, y, core).
Axes of the slice: x: 2, y: 2, z: 4, core: 2. Of those that a mesh axis runs over, the one named last changes fastest.
Arguments:
- embeddings: bfloat16 [8192, 1024], P(('parts', 'blk')), parts along dimension 0, may hold values from -6 to 6
- cluster: int32 [8192, 1], P(('parts', 'blk')), parts along dimension 0, may hold values from 0 to 15; in each aligned block of 256 rows (0 to 255, 256 to 511, ...) at most 32 rows name the same one
- rank: int32 [8192], P(('parts', 'blk')), parts along dimension 0, may hold values from 0 to 4095, each once
Outputs:
- best: float32 [8192], P(('parts', 'blk')), parts along dimension 0
There are 2 independent parts, one for each index of `parts`. A program takes and returns all parts, laid end to end along the dimension named above; each array names one. Nothing has to cross between parts.
Inputs may be any that keep to these rules, and one draw needn't show every extreme that they name: Cluster c is kept by index c of blk. The rows of one device name one cluster at most 32 times, a bound that some block reaches. Each rank appears once in a group.
All inputs are finite; a program needn't handle non-finite values.
Results may differ from a plain program's by a relative error of at most 0.0013.
Values may be sent and summed in bfloat16 or wider, within the bound.
A program may use at most 64 MiB of HBM per device.

v0:
```python
import functools

import jax
import jax.numpy as jnp
from jax import lax
from jax.experimental import pallas as pl
from jax.experimental.pallas import tpu as pltpu
from jax.sharding import PartitionSpec as P

MESH = pl.DeviceIdType.MESH
HIGHEST = lax.Precision.HIGHEST


def best_over(q_rows, q_rank, k_rows, k_rank):
    total = q_rows.shape[0]
    block_len = min(512, total)
    similar = lax.dot_general(
        q_rows, k_rows, (((1,), (1,)), ((), ())), preferred_element_type=jnp.float32
    )
    allowed = k_rank[None, :] > q_rank[0:block_len, None]
    pieces = jnp.max(jnp.where(allowed, similar, -1.0), axis=1)
    return pieces


def local(embeddings, cluster, rank):
    devices = lax.axis_size("blk")
    local_rows = embeddings.shape[0]
    width = embeddings.shape[1]
    slot_total = 2 * local_rows
    capacity = slot_total // devices
    floats = embeddings.astype(jnp.float32)
    unit_rows = (
        floats * lax.rsqrt(jnp.sum(floats * floats, axis=1, keepdims=True) + 1e-06)
    ).astype(jnp.bfloat16)
    target = cluster[:, 0]
    one_hot = (target[:, None] == jnp.arange(devices, dtype=jnp.int32)[None, :]).astype(jnp.int32)
    earlier = jnp.cumsum(one_hot, axis=0) - one_hot
    within = jnp.sum(earlier * one_hot, axis=1)
    slot_of = target * capacity + within
    send_rows = (
        jnp.zeros((slot_total, width), jnp.bfloat16)
        .at[slot_of]
        .set(unit_rows)
        .reshape(devices, capacity, width)
    )
    send_rank = (
        jnp.full((slot_total,), -1, jnp.int32).at[slot_of].set(rank).reshape(devices, capacity)
    )
    got_rows, got_rank = (
        lax.all_to_all(send_rows, "blk", split_axis=0, concat_axis=0, tiled=True),
        lax.all_to_all(send_rank, "blk", split_axis=0, concat_axis=0, tiled=True),
    )
    all_rows = got_rows.reshape(slot_total, width)
    all_rank = got_rank.reshape(slot_total)
    best_flat = best_over(all_rows, all_rank, all_rows, all_rank)
    returned = lax.all_to_all(
        best_flat.reshape(devices, capacity), "blk", split_axis=0, concat_axis=0, tiled=True
    )
    return returned.reshape(slot_total)[slot_of]


def kernel(
    n, cap, emb_hbm, cluster_hbm, rank_hbm, out_ref,
    emb, cluster_ref, rank_ref, send_rows, rows, send_rank, ranks, send_best, bests,
    load_sems, row_out, row_in, rank_out, rank_in, best_out, best_in,
):
    me = lax.axis_index("blk")
    count, width = emb.shape
    slots = n * cap
    half = n // 2
    side = me // half
    spot = me % half
    far = (1 - side) * half
    near = side * half

    barrier = pltpu.get_barrier_semaphore()
    loads = [
        pltpu.make_async_copy(source, into, load_sems.at[i])
        for i, (source, into) in enumerate(
            [(cluster_hbm, cluster_ref), (rank_hbm, rank_ref), (emb_hbm, emb)]
        )
    ]
    for load in loads:
        load.start()

    @pl.loop(1, n)
    def _(k):
        pl.semaphore_signal(
            barrier, inc=1, device_id={"blk": lax.rem(me + k, n)}, device_id_type=MESH
        )

    loads[0].wait()
    loads[1].wait()
    target = cluster_ref[...]
    ids = lax.broadcasted_iota(jnp.int32, (n, count), 0)
    named = (ids == target).astype(jnp.float32)
    before = lax.broadcasted_iota(jnp.int32, (count, count), 0)
    after = lax.broadcasted_iota(jnp.int32, (count, count), 1)
    upper = (before < after).astype(jnp.bfloat16)
    earlier = jnp.dot(named.astype(jnp.bfloat16), upper, preferred_element_type=jnp.float32)
    within = jnp.sum(earlier * named, axis=0, keepdims=True).astype(jnp.int32)
    slot_of = target * cap + within
    lanes = lax.broadcasted_iota(jnp.int32, (128, count), 0)
    spots = (lanes == within).astype(jnp.float32)
    placed = lax.dot_general(
        named * (rank_ref[...] + 1).astype(jnp.float32), spots, (((1,), (1,)), ((), ())),
        precision=HIGHEST, preferred_element_type=jnp.float32,
    )
    for c in range(n):
        send_rank[c] = placed[c:c + 1]

    loads[2].wait()
    floats = emb[...].astype(jnp.float32)
    unit = (
        floats * lax.rsqrt(jnp.sum(floats * floats, axis=1, keepdims=True) + 1e-06)
    ).astype(jnp.bfloat16)

    def pack(first):
        wanted = lax.broadcasted_iota(jnp.int32, (half * cap, count), 0) + first * cap
        pick = (wanted == slot_of).astype(jnp.bfloat16)
        packed = jnp.dot(pick, unit, preferred_element_type=jnp.float32).astype(jnp.bfloat16)
        send_rows[pl.ds(first, half)] = packed.reshape(half, cap, width)

    def row_copy(to):
        return pltpu.make_async_remote_copy(
            src_ref=send_rows.at[to], dst_ref=rows.at[me], send_sem=row_out.at[to],
            recv_sem=row_in.at[me], device_id={"blk": to}, device_id_type=MESH,
        )

    def row_arrival(source):
        return pltpu.make_async_remote_copy(
            src_ref=send_rows.at[source], dst_ref=rows.at[source], send_sem=row_out.at[source],
            recv_sem=row_in.at[source], device_id={"blk": source}, device_id_type=MESH,
        )

    def rank_copy(to, at):
        return pltpu.make_async_remote_copy(
            src_ref=send_rank.at[to], dst_ref=ranks.at[at], send_sem=rank_out.at[to],
            recv_sem=rank_in.at[at], device_id={"blk": to}, device_id_type=MESH,
        )

    def best_copy(to, at):
        return pltpu.make_async_remote_copy(
            src_ref=send_best, dst_ref=bests.at[at], send_sem=best_out.at[to],
            recv_sem=best_in.at[at], device_id={"blk": to}, device_id_type=MESH,
        )

    pack(far)
    pl.semaphore_wait(barrier, n - 1)

    @pl.loop(1, n)
    def _(k):
        rank_copy(lax.rem(me + k, n), me).start()

    quarter = n // 4
    turn = me % quarter
    outer = (1 - side) * 3 * quarter
    inner = (2 - side) * quarter
    own = me - turn
    sibling = side * half + (1 - spot // quarter) * quarter
    early = quarter // 2

    def send(first, begin, end):
        @pl.loop(begin, end)
        def _(k):
            row_copy(first + lax.rem(turn + k, quarter)).start()

    send(outer, 0, quarter)
    send(inner, 0, early)
    pack(near)
    send(own, 1, quarter)
    rows[me] = send_rows[me]

    @pl.loop(0, quarter)
    def _(k):
        row_copy(outer + k).wait_send()

    send(sibling, 0, quarter)
    send(inner, early, quarter)
    ranks[me] = send_rank[me]

    @pl.loop(1, n)
    def _(k):
        at = lax.rem(me + k, n)
        rank_copy(at, at).wait()

    held = jnp.concatenate([ranks[c] for c in range(n)], axis=0)
    source = lax.broadcasted_iota(jnp.int32, (n, slots), 0)
    slot = lax.broadcasted_iota(jnp.int32, (n, slots), 1)
    spread = (slot // cap == source).astype(jnp.float32)
    across = lax.dot_general(
        held, spread, (((0,), (0,)), ((), ())),
        precision=HIGHEST, preferred_element_type=jnp.float32,
    )
    lane_of = lax.broadcasted_iota(jnp.int32, (128, slots), 0)
    slot_in = lax.broadcasted_iota(jnp.int32, (128, slots), 1) % cap
    rank_row = jnp.sum(jnp.where(lane_of == slot_in, across, 0.0), axis=0, keepdims=True)
    down = lax.dot_general(
        spread, held, (((0,), (0,)), ((), ())),
        precision=HIGHEST, preferred_element_type=jnp.float32,
    )
    lane_at = lax.broadcasted_iota(jnp.int32, (slots, 128), 1)
    slot_at = lax.broadcasted_iota(jnp.int32, (slots, 128), 0) % cap
    rank_col = jnp.sum(jnp.where(lane_at == slot_at, down, 0.0), axis=1, keepdims=True)

    @pl.loop(1, n)
    def _(k):
        row_arrival(lax.rem(me + k, n)).wait_recv()

    everyone = rows[...].reshape(slots, width)
    similar = lax.dot_general(
        everyone, everyone, (((1,), (1,)), ((), ())), preferred_element_type=jnp.float32
    )
    best = jnp.max(jnp.where(rank_col > rank_row, similar, -1.0), axis=0, keepdims=True)
    for k in range(slots // 128):
        send_best[k:k + 1] = best[:, 128 * k:128 * (k + 1)]
    bests[me] = send_best[...]

    @pl.loop(1, n)
    def _(k):
        best_copy(lax.rem(me + k, n), me).start()

    @pl.loop(0, quarter)
    def _(k):
        row_copy(inner + k).wait_send()
        row_copy(sibling + k).wait_send()

    @pl.loop(1, quarter)
    def _(k):
        row_copy(own + lax.rem(turn + k, quarter)).wait_send()

    @pl.loop(1, n)
    def _(k):
        at = lax.rem(me + k, n)
        best_copy(at, at).wait()

    per = 128 // cap
    mine = jnp.concatenate([bests[c, pl.ds(me // per, 1)] for c in range(n)], axis=0)
    by_row = lax.dot_general(
        mine, named, (((0,), (0,)), ((), ())),
        precision=HIGHEST, preferred_element_type=jnp.float32,
    )
    place = (me % per) * cap + within
    out_ref[...] = jnp.sum(jnp.where(lanes == place, by_row, 0.0), axis=0, keepdims=True)


def fused(embeddings, cluster, rank):
    n = lax.axis_size("blk")
    count, width = embeddings.shape
    cap = 2 * count // n
    vmem = pl.BlockSpec(memory_space=pltpu.VMEM)
    best = pl.pallas_call(
        functools.partial(kernel, n, cap),
        out_shape=pltpu.VMEM((1, count), jnp.float32),
        in_specs=[pl.BlockSpec(memory_space=pl.ANY)] * 3,
        out_specs=vmem,
        scratch_shapes=[
            pltpu.VMEM((count, width), jnp.bfloat16),
            pltpu.VMEM((1, count), jnp.int32),
            pltpu.VMEM((1, count), jnp.int32),
            pltpu.VMEM((n, cap, width), jnp.bfloat16),
            pltpu.VMEM((n, cap, width), jnp.bfloat16),
            pltpu.VMEM((n, 1, 128), jnp.float32),
            pltpu.VMEM((n, 1, 128), jnp.float32),
            pltpu.VMEM((8, 128), jnp.float32),
            pltpu.VMEM((n, 8, 128), jnp.float32),
            pltpu.SemaphoreType.DMA((3,)),
        ] + [pltpu.SemaphoreType.DMA((n,))] * 6,
        compiler_params=pltpu.CompilerParams(collective_id=0, has_side_effects=True),
    )(embeddings, cluster.reshape(1, count), rank.reshape(1, count))
    return best.reshape(count)


def solution(mesh):
    def body(embeddings, cluster, rank):
        n = lax.axis_size("blk")
        slots = 2 * embeddings.shape[0]
        cap = slots // n
        if n % 4 == 0 and slots == 512 and cap % 16 == 0 and 128 % cap == 0:
            return fused(embeddings, cluster, rank)
        return local(embeddings, cluster, rank)

    return jax.shard_map(
        body,
        mesh=mesh,
        in_specs=(P(("parts", "blk"), None), P(("parts", "blk"), None), P(("parts", "blk"))),
        out_specs=P(("parts", "blk")),
        check_vma=False,
    )
```

profile of v0, /device:TPU:0, one launch (start us, length us, event | category | flops | bytes accessed | tf_op | source)
XLA Modules:
  0.0 36.1 jit_solution(16401607452076687130)
XLA Ops:
  0.0 35.5 %shard_map.37 = f32[1,256]{1,0:T(1,128)S(1)} custom-call(bf16[256,1024]{1,0:T(8,128)(2,1)} %emb_hbm.1, s32[1,256]{1,0:T(1,128)} %bitcast.4, s32[1,256]{1,0:T(1,128)} %bitcast.5), custom_call_target="tpu_custom_call" | custom-call | tf_op jit(solution)/shard_map/pallas_call | solution.py:252
  35.5 0.6 %copy.5 = f32[256]{0:T(256)} copy(f32[256]{0:T(256)S(1)} %bitcast.3) | data formatting | bytes 2048
where the time goes:
time: 36.2 us; the launch traced here: 36.1 us
  Pallas kernels  35.5 us (98%)
  local copies, waits for them, and re-layouts  0.56 us (2%)
    pallas_call x1, Pallas kernels, fused(): pl.pallas_call(functools.partial(kernel, n, cap), out_shape=pltpu.VMEM((1...  35.5 us

commit v1 on v0

v1 whole, which is shorter than its diff:
```python
import functools

import jax
import jax.numpy as jnp
from jax import lax
from jax.experimental import pallas as pl
from jax.experimental.pallas import tpu as pltpu
from jax.sharding import PartitionSpec as P

MESH = pl.DeviceIdType.MESH
HIGHEST = lax.Precision.HIGHEST


def best_over(q_rows, q_rank, k_rows, k_rank):
    total = q_rows.shape[0]
    block_len = min(512, total)
    similar = lax.dot_general(
        q_rows, k_rows, (((1,), (1,)), ((), ())), preferred_element_type=jnp.float32
    )
    allowed = k_rank[None, :] > q_rank[0:block_len, None]
    pieces = jnp.max(jnp.where(allowed, similar, -1.0), axis=1)
    return pieces


def local(embeddings, cluster, rank):
    devices = lax.axis_size("blk")
    local_rows = embeddings.shape[0]
    width = embeddings.shape[1]
    slot_total = 2 * local_rows
    capacity = slot_total // devices
    floats = embeddings.astype(jnp.float32)
    unit_rows = (
        floats * lax.rsqrt(jnp.sum(floats * floats, axis=1, keepdims=True) + 1e-06)
    ).astype(jnp.bfloat16)
    target = cluster[:, 0]
    one_hot = (target[:, None] == jnp.arange(devices, dtype=jnp.int32)[None, :]).astype(jnp.int32)
    earlier = jnp.cumsum(one_hot, axis=0) - one_hot
    within = jnp.sum(earlier * one_hot, axis=1)
    slot_of = target * capacity + within
    send_rows = (
        jnp.zeros((slot_total, width), jnp.bfloat16)
        .at[slot_of]
        .set(unit_rows)
        .reshape(devices, capacity, width)
    )
    send_rank = (
        jnp.full((slot_total,), -1, jnp.int32).at[slot_of].set(rank).reshape(devices, capacity)
    )
    got_rows, got_rank = (
        lax.all_to_all(send_rows, "blk", split_axis=0, concat_axis=0, tiled=True),
        lax.all_to_all(send_rank, "blk", split_axis=0, concat_axis=0, tiled=True),
    )
    all_rows = got_rows.reshape(slot_total, width)
    all_rank = got_rank.reshape(slot_total)
    best_flat = best_over(all_rows, all_rank, all_rows, all_rank)
    returned = lax.all_to_all(
        best_flat.reshape(devices, capacity), "blk", split_axis=0, concat_axis=0, tiled=True
    )
    return returned.reshape(slot_total)[slot_of]


def kernel(
    n, cap, emb_hbm, cluster_hbm, rank_hbm, out_ref,
    emb, cluster_ref, rank_ref, send_rows, rows, send_rank, ranks, send_best, bests,
    load_sems, row_out, row_in, rank_out, rank_in, best_out, best_in, edge_in, half_in, all_in,
):
    me = lax.axis_index("blk")
    count, width = emb.shape
    slots = n * cap
    quarter = n // 4
    part = quarter * cap
    early = quarter // 2
    layer = me // quarter
    turn = me % quarter
    side = layer // 2
    middle = jnp.logical_or(layer == 1, layer == 2)
    near = 1 + layer % 2
    rim = 3 * side
    far_rim = 3 - rim
    last = 2 - side
    inward = near * quarter
    across = last * quarter
    own = me - turn

    barrier = pltpu.get_barrier_semaphore()
    loads = [
        pltpu.make_async_copy(source, into, load_sems.at[i])
        for i, (source, into) in enumerate(
            [(cluster_hbm, cluster_ref), (rank_hbm, rank_ref), (emb_hbm, emb)]
        )
    ]

    def signal(sem, to):
        pl.semaphore_signal(sem, inc=1, device_id={"blk": to}, device_id_type=MESH)

    @pl.when(middle)
    def _():
        @pl.loop(0, quarter)
        def _(k):
            signal(barrier, inward + k)

        @pl.loop(0, quarter)
        def _(k):
            signal(barrier, rim * quarter + k)

        @pl.loop(1, quarter)
        def _(k):
            signal(barrier, own + lax.rem(turn + k, quarter))

    for load in loads:
        load.start()

    loads[0].wait()
    target = cluster_ref[...]
    ids = lax.broadcasted_iota(jnp.int32, (n, count), 0)
    named = (ids == target).astype(jnp.float32)
    before = lax.broadcasted_iota(jnp.int32, (count, count), 0)
    after = lax.broadcasted_iota(jnp.int32, (count, count), 1)
    upper = (before < after).astype(jnp.bfloat16)
    earlier = jnp.dot(named.astype(jnp.bfloat16), upper, preferred_element_type=jnp.float32)
    within = jnp.sum(earlier * named, axis=0, keepdims=True).astype(jnp.int32)
    slot_of = target * cap + within
    loads[2].wait()

    def pack(to):
        wanted = lax.broadcasted_iota(jnp.int32, (cap, count), 0) + to * cap
        pick = (wanted == slot_of).astype(jnp.bfloat16)
        floats = jnp.dot(pick, emb[...], preferred_element_type=jnp.float32)
        scale = lax.rsqrt(jnp.sum(floats * floats, axis=1, keepdims=True) + 1e-06)
        send_rows[to] = (floats * scale).astype(jnp.bfloat16)

    def row_copy(to):
        return pltpu.make_async_remote_copy(
            src_ref=send_rows.at[to], dst_ref=rows.at[me], send_sem=row_out.at[to],
            recv_sem=row_in.at[me], device_id={"blk": to}, device_id_type=MESH,
        )

    def row_arrival(source):
        return pltpu.make_async_remote_copy(
            src_ref=send_rows.at[source], dst_ref=rows.at[source], send_sem=row_out.at[source],
            recv_sem=row_in.at[source], device_id={"blk": source}, device_id_type=MESH,
        )

    def rank_copy(to, at):
        return pltpu.make_async_remote_copy(
            src_ref=send_rank.at[to], dst_ref=ranks.at[at], send_sem=rank_out.at[to],
            recv_sem=rank_in.at[at], device_id={"blk": to}, device_id_type=MESH,
        )

    per = 128 // cap

    def best_copy(to, at):
        return pltpu.make_async_remote_copy(
            src_ref=send_best.at[to // per], dst_ref=bests.at[at], send_sem=best_out.at[to],
            recv_sem=best_in.at[at], device_id={"blk": to}, device_id_type=MESH,
        )

    def turned(k):
        return lax.rem(turn + k, quarter)

    def pack_all(first, begin, end):
        @pl.loop(begin, end)
        def _(k):
            pack(first + turned(k))

    def send_all(first, begin, end):
        @pl.loop(begin, end)
        def _(k):
            row_copy(first + turned(k)).start()

    def pack_send(first, begin, end):
        @pl.loop(begin, end)
        def _(k):
            to = first + turned(k)
            pack(to)
            row_copy(to).start()

    pack(inward + turn)

    @pl.when(middle)
    def _():
        pl.semaphore_wait(barrier, 2 * quarter - 1)

    @pl.when(jnp.logical_not(middle))
    def _():
        pl.semaphore_wait(barrier, quarter)

        @pl.loop(0, quarter)
        def _(k):
            signal(edge_in, inward + k)

    row_copy(inward + turn).start()
    pack_send(inward, 1, early)
    loads[1].wait()
    lanes = lax.broadcasted_iota(jnp.int32, (128, count), 0)
    spots = (lanes == within).astype(jnp.float32)
    placed = lax.dot_general(
        named * (rank_ref[...] + 1).astype(jnp.float32), spots, (((1,), (1,)), ((), ())),
        precision=HIGHEST, preferred_element_type=jnp.float32,
    )
    for c in range(n):
        send_rank[c] = placed[c:c + 1]

    def rank_all(first, begin):
        @pl.loop(begin, quarter)
        def _(k):
            rank_copy(first + turned(k), me).start()

    rank_all(inward, 0)

    @pl.when(middle)
    def _():
        rank_all(own, 1)
        pack_send(own, 1, quarter)
        pl.semaphore_wait(edge_in, quarter)
        signal(half_in, inward + turn)
        rank_all(rim * quarter, 0)
        pack_all(far_rim * quarter, 0, quarter)
        pl.semaphore_wait(half_in, 1)
        signal(all_in, rim * quarter + turn)
        rank_all(far_rim * quarter, 0)
        send_all(far_rim * quarter, 0, quarter)
        pack_send(rim * quarter, 0, quarter)
        pack_send(inward, early, quarter)

    @pl.when(jnp.logical_not(middle))
    def _():
        pack_send(inward, early, quarter)
        pack_all(far_rim * quarter, 0, quarter)
        pack_all(own, 1, quarter)
        pl.semaphore_wait(all_in, 1)
        rank_all(own, 1)
        rank_all(far_rim * quarter, 0)
        rank_all(across, 0)
        send_all(far_rim * quarter, 0, quarter)
        send_all(own, 1, quarter)
        pack_send(across, 0, quarter)

    pack(me)
    rows[me] = send_rows[me]
    ranks[me] = send_rank[me]

    @pl.loop(1, n)
    def _(k):
        at = lax.rem(me + k, n)
        rank_copy(at, at).wait()

    order = [0, 1 + side, 3, last]
    held = jnp.concatenate(
        [ranks[g * quarter + k] for g in order for k in range(quarter)], axis=0
    )
    source = lax.broadcasted_iota(jnp.int32, (n, slots), 0)
    slot = lax.broadcasted_iota(jnp.int32, (n, slots), 1)
    spread = (slot // cap == source).astype(jnp.float32)
    wide = lax.dot_general(
        held, spread, (((0,), (0,)), ((), ())),
        precision=HIGHEST, preferred_element_type=jnp.float32,
    )
    lane_of = lax.broadcasted_iota(jnp.int32, (128, slots), 0)
    slot_in = lax.broadcasted_iota(jnp.int32, (128, slots), 1) % cap
    rank_row = jnp.sum(jnp.where(lane_of == slot_in, wide, 0.0), axis=0, keepdims=True)
    down = lax.dot_general(
        spread, held, (((0,), (0,)), ((), ())),
        precision=HIGHEST, preferred_element_type=jnp.float32,
    )
    lane_at = lax.broadcasted_iota(jnp.int32, (slots, 128), 1)
    slot_at = lax.broadcasted_iota(jnp.int32, (slots, 128), 0) % cap
    rank_col = jnp.sum(jnp.where(lane_at == slot_at, down, 0.0), axis=1, keepdims=True)

    @pl.loop(0, n)
    def _(k):
        @pl.when(jnp.logical_and(k != me, k // quarter != last))
        def _():
            row_arrival(k).wait_recv()

    def group(g):
        return rows[pl.ds(g * quarter, quarter)].reshape(part, width)

    def best_of(keys, key_rank, queries, query_rank):
        similar = lax.dot_general(
            keys, queries, (((1,), (1,)), ((), ())), preferred_element_type=jnp.float32
        )
        return jnp.max(jnp.where(key_rank > query_rank, similar, -1.0), axis=0, keepdims=True)

    head = 3 * part
    first = jnp.concatenate([group(g) for g in order[:3]], axis=0)
    best_first = best_of(first, rank_col[:head], first, rank_row[:, :head])

    @pl.loop(0, quarter)
    def _(k):
        row_arrival(across + k).wait_recv()

    tail = group(last)
    best_first = jnp.maximum(
        best_first, best_of(tail, rank_col[head:], first, rank_row[:, :head])
    )
    best_tail = jnp.maximum(
        best_of(first, rank_col[:head], tail, rank_row[:, head:]),
        best_of(tail, rank_col[head:], tail, rank_row[:, head:]),
    )
    for i, g in enumerate(order[:3]):
        send_best[g] = best_first[:, part * i:part * (i + 1)]
    send_best[last] = best_tail

    @pl.loop(0, n)
    def _(to):
        @pl.when(to != me)
        def _():
            best_copy(to, me).start()

    bests[me] = send_best[me // per]

    @pl.loop(0, n)
    def _(to):
        @pl.when(to != me)
        def _():
            row_copy(to).wait_send()

    @pl.loop(1, n)
    def _(k):
        at = lax.rem(me + k, n)
        best_copy(at, at).wait()

    mine = jnp.concatenate([bests[c] for c in range(n)], axis=0)
    place = (me % per) * cap + within
    for k in range(count // 128):
        piece = slice(128 * k, 128 * (k + 1))
        at = jnp.broadcast_to(place[:, piece], (n, 128))
        found = jnp.take_along_axis(mine, at, axis=1, mode="promise_in_bounds")
        out_ref[:, piece] = jnp.sum(
            jnp.where(named[:, piece] > 0.0, found, 0.0), axis=0, keepdims=True
        )


def fused(embeddings, cluster, rank):
    n = lax.axis_size("blk")
    count, width = embeddings.shape
    cap = 2 * count // n
    slots = n * cap
    vmem = pl.BlockSpec(memory_space=pltpu.VMEM)
    best = pl.pallas_call(
        functools.partial(kernel, n, cap),
        out_shape=pltpu.VMEM((1, count), jnp.float32),
        in_specs=[pl.BlockSpec(memory_space=pl.ANY)] * 3,
        out_specs=vmem,
        scratch_shapes=[
            pltpu.VMEM((count, width), jnp.bfloat16),
            pltpu.VMEM((1, count), jnp.int32),
            pltpu.VMEM((1, count), jnp.int32),
            pltpu.VMEM((n, cap, width), jnp.bfloat16),
            pltpu.VMEM((n, cap, width), jnp.bfloat16),
            pltpu.VMEM((n, 1, 128), jnp.float32),
            pltpu.VMEM((n, 1, 128), jnp.float32),
            pltpu.VMEM((slots // 128, 1, 128), jnp.float32),
            pltpu.VMEM((n, 1, 128), jnp.float32),
            pltpu.SemaphoreType.DMA((3,)),
        ] + [pltpu.SemaphoreType.DMA((n,))] * 6 + [pltpu.SemaphoreType.REGULAR] * 3,
        compiler_params=pltpu.CompilerParams(collective_id=0, has_side_effects=True),
    )(embeddings, cluster.reshape(1, count), rank.reshape(1, count))
    return best.reshape(count)


def solution(mesh):
    def body(embeddings, cluster, rank):
        n = lax.axis_size("blk")
        slots = 2 * embeddings.shape[0]
        cap = slots // n
        if n % 4 == 0 and slots == 512 and n // 4 * cap == 128:
            return fused(embeddings, cluster, rank)
        return local(embeddings, cluster, rank)

    return jax.shard_map(
        body,
        mesh=mesh,
        in_specs=(P(("parts", "blk"), None), P(("parts", "blk"), None), P(("parts", "blk"))),
        out_specs=P(("parts", "blk")),
        check_vma=False,
    )
```

time: 36.2 us -> 35 us (0.967)
  Pallas kernels: 35.5 us -> 34.3 us
    pallas_call x1, Pallas kernels: 35.5 us -> 34.3 us  [fused(): pl.pallas_call(functools.partial(kernel, n, cap), out_shape=pltpu.VMEM((1...]
where the time goes in v1:
time: 35 us; the launch traced here: 34.8 us
  Pallas kernels  34.3 us (98%)
  local copies, waits for them, and re-layouts  0.56 us (2%)
    pallas_call x1, Pallas kernels, fused(): pl.pallas_call(functools.partial(kernel, n, cap), out_shape=pltpu.VMEM((1...  34.3 us

profile of v1, /device:TPU:0, one launch (start us, length us, event | category | flops | bytes accessed | tf_op | source)
XLA Modules:
  0.0 34.8 jit_solution(11013050918550168224)
XLA Ops:
  0.0 34.3 %shard_map.37 = f32[1,256]{1,0:T(1,128)S(1)} custom-call(bf16[256,1024]{1,0:T(8,128)(2,1)} %emb_hbm.1, s32[1,256]{1,0:T(1,128)} %bitcast.4, s32[1,256]{1,0:T(1,128)} %bitcast.5), custom_call_target="tpu_custom_call" | custom-call | tf_op jit(solution)/shard_map/pallas_call | solution.py:341
  34.3 0.6 %copy.5 = f32[256]{0:T(256)} copy(f32[256]{0:T(256)S(1)} %bitcast.3) | data formatting | bytes 2048

commit v2 on v1

--- a/solution.py
+++ b/solution.py
@@ -69,10 +69,10 @@
     slots = n * cap
     quarter = n // 4
     part = quarter * cap
-    early = quarter // 2
     layer = me // quarter
     turn = me % quarter
     side = layer // 2
+    early = quarter - 1
     middle = jnp.logical_or(layer == 1, layer == 2)
     near = 1 + layer % 2
     rim = 3 * side
@@ -90,6 +90,9 @@
         )
     ]
 
+    for load in loads:
+        load.start()
+
     def signal(sem, to):
         pl.semaphore_signal(sem, inc=1, device_id={"blk": to}, device_id_type=MESH)
 
@@ -106,9 +109,6 @@
         @pl.loop(1, quarter)
         def _(k):
             signal(barrier, own + lax.rem(turn + k, quarter))
-
-    for load in loads:
-        load.start()
 
     loads[0].wait()
     target = cluster_ref[...]
@@ -120,43 +120,52 @@
     earlier = jnp.dot(named.astype(jnp.bfloat16), upper, preferred_element_type=jnp.float32)
     within = jnp.sum(earlier * named, axis=0, keepdims=True).astype(jnp.int32)
     slot_of = target * cap + within
-    loads[2].wait()
-
-    def pack(to):
+    def choose(to):
         wanted = lax.broadcasted_iota(jnp.int32, (cap, count), 0) + to * cap
-        pick = (wanted == slot_of).astype(jnp.bfloat16)
+        return (wanted == slot_of).astype(jnp.bfloat16)
+
+    def pack(to, pick=None):
+        pick = choose(to) if pick is None else pick
         floats = jnp.dot(pick, emb[...], preferred_element_type=jnp.float32)
         scale = lax.rsqrt(jnp.sum(floats * floats, axis=1, keepdims=True) + 1e-06)
         send_rows[to] = (floats * scale).astype(jnp.bfloat16)
 
-    def row_copy(to):
+    def place_of(source, keeper):
+        z = source // quarter
+        end = 2 - keeper // (2 * quarter)
+        step = source % quarter
+        wait = lax.rem(step - keeper % quarter + 2 + quarter, quarter)
+        return jnp.where(z == end, 3 * quarter + wait, (z + 1) // 2 * quarter + step)
+
+    def row_copy(to, at=None):
+        at = place_of(me, to) if at is None else at
         return pltpu.make_async_remote_copy(
-            src_ref=send_rows.at[to], dst_ref=rows.at[me], send_sem=row_out.at[to],
-            recv_sem=row_in.at[me], device_id={"blk": to}, device_id_type=MESH,
-        )
-
-    def row_arrival(source):
-        return pltpu.make_async_remote_copy(
-            src_ref=send_rows.at[source], dst_ref=rows.at[source], send_sem=row_out.at[source],
-            recv_sem=row_in.at[source], device_id={"blk": source}, device_id_type=MESH,
-        )
-
-    def rank_copy(to, at):
+            src_ref=send_rows.at[to], dst_ref=rows.at[at], send_sem=row_out.at[to],
+            recv_sem=row_in.at[at], device_id={"blk": to}, device_id_type=MESH,
+        )
+
+    def rank_copy(to, at=None):
+        at = place_of(me, to) if at is None else at
         return pltpu.make_async_remote_copy(
             src_ref=send_rank.at[to], dst_ref=ranks.at[at], send_sem=rank_out.at[to],
             recv_sem=rank_in.at[at], device_id={"blk": to}, device_id_type=MESH,
         )
 
+    other = lax.rem(me + 1, n)
+    home = place_of(me, me)
+
     per = 128 // cap
 
     def best_copy(to, at):
         return pltpu.make_async_remote_copy(
-            src_ref=send_best.at[to // per], dst_ref=bests.at[at], send_sem=best_out.at[to],
+            src_ref=send_best.at[place_of(to, me) // per], dst_ref=bests.at[at], send_sem=best_out.at[to],
             recv_sem=best_in.at[at], device_id={"blk": to}, device_id_type=MESH,
         )
 
     def turned(k):
-        return lax.rem(turn + k, quarter)
+        odd = turn % 2
+        cross = (1 - odd) * lax.rem(k + 1, 2) + odd * lax.rem((k + 1) // 2, 2)
+        return lax.rem(turn // 2 + cross, 2) * 2 + lax.rem(turn + k // 2, 2)
 
     def pack_all(first, begin, end):
         @pl.loop(begin, end)
@@ -175,7 +184,10 @@
             pack(to)
             row_copy(to).start()
 
-    pack(inward + turn)
+    lead = inward + turned(0)
+    pick_lead = choose(lead)
+    loads[2].wait()
+    pack(lead, pick_lead)
 
     @pl.when(middle)
     def _():
@@ -189,8 +201,8 @@
         def _(k):
             signal(edge_in, inward + k)
 
-    row_copy(inward + turn).start()
-    pack_send(inward, 1, early)
+    row_copy(lead).start()
+    pack_send(inward, 1, 2)
     loads[1].wait()
     lanes = lax.broadcasted_iota(jnp.int32, (128, count), 0)
     spots = (lanes == within).astype(jnp.float32)
@@ -204,51 +216,59 @@
     def rank_all(first, begin):
         @pl.loop(begin, quarter)
         def _(k):
-            rank_copy(first + turned(k), me).start()
+            rank_copy(first + lax.rem(turn + k, quarter)).start()
+
+    def send_own():
+        @pl.loop(1, quarter)
+        def _(k):
+            to = own + lax.rem(turn + k, quarter)
+            pack(to)
+            row_copy(to).start()
 
     rank_all(inward, 0)
 
     @pl.when(middle)
     def _():
-        rank_all(own, 1)
-        pack_send(own, 1, quarter)
         pl.semaphore_wait(edge_in, quarter)
         signal(half_in, inward + turn)
+        pack_send(inward, 2, early)
         rank_all(rim * quarter, 0)
-        pack_all(far_rim * quarter, 0, quarter)
+        rank_all(own, 1)
+        pack_send(rim * quarter, 0, quarter)
         pl.semaphore_wait(half_in, 1)
         signal(all_in, rim * quarter + turn)
         rank_all(far_rim * quarter, 0)
-        send_all(far_rim * quarter, 0, quarter)
-        pack_send(rim * quarter, 0, quarter)
+        pack_send(far_rim * quarter, 0, quarter)
         pack_send(inward, early, quarter)
+        send_own()
 
     @pl.when(jnp.logical_not(middle))
     def _():
-        pack_send(inward, early, quarter)
+        pack_send(inward, 2, quarter)
         pack_all(far_rim * quarter, 0, quarter)
-        pack_all(own, 1, quarter)
         pl.semaphore_wait(all_in, 1)
-        rank_all(own, 1)
         rank_all(far_rim * quarter, 0)
         rank_all(across, 0)
+        rank_all(own, 1)
         send_all(far_rim * quarter, 0, quarter)
-        send_all(own, 1, quarter)
         pack_send(across, 0, quarter)
+        send_own()
 
     pack(me)
-    rows[me] = send_rows[me]
-    ranks[me] = send_rank[me]
+    rows[home] = send_rows[me]
+    ranks[home] = send_rank[me]
 
     @pl.loop(1, n)
     def _(k):
-        at = lax.rem(me + k, n)
-        rank_copy(at, at).wait()
-
-    order = [0, 1 + side, 3, last]
-    held = jnp.concatenate(
-        [ranks[g * quarter + k] for g in order for k in range(quarter)], axis=0
-    )
+        rank_copy(lax.rem(me + k, n)).wait_send()
+
+    @pl.loop(0, n)
+    def _(k):
+        @pl.when(k != home)
+        def _():
+            rank_copy(other, k).wait_recv()
+
+    held = jnp.concatenate([ranks[c] for c in range(n)], axis=0)
     source = lax.broadcasted_iota(jnp.int32, (n, slots), 0)
     slot = lax.broadcasted_iota(jnp.int32, (n, slots), 1)
     spread = (slot // cap == source).astype(jnp.float32)
@@ -267,48 +287,57 @@
     slot_at = lax.broadcasted_iota(jnp.int32, (slots, 128), 0) % cap
     rank_col = jnp.sum(jnp.where(lane_at == slot_at, down, 0.0), axis=1, keepdims=True)
 
-    @pl.loop(0, n)
-    def _(k):
-        @pl.when(jnp.logical_and(k != me, k // quarter != last))
-        def _():
-            row_arrival(k).wait_recv()
-
-    def group(g):
-        return rows[pl.ds(g * quarter, quarter)].reshape(part, width)
-
     def best_of(keys, key_rank, queries, query_rank):
         similar = lax.dot_general(
             keys, queries, (((1,), (1,)), ((), ())), preferred_element_type=jnp.float32
         )
         return jnp.max(jnp.where(key_rank > query_rank, similar, -1.0), axis=0, keepdims=True)
 
-    head = 3 * part
-    first = jnp.concatenate([group(g) for g in order[:3]], axis=0)
-    best_first = best_of(first, rank_col[:head], first, rank_row[:, :head])
-
-    @pl.loop(0, quarter)
-    def _(k):
-        row_arrival(across + k).wait_recv()
-
-    tail = group(last)
-    best_first = jnp.maximum(
-        best_first, best_of(tail, rank_col[head:], first, rank_row[:, :head])
-    )
-    best_tail = jnp.maximum(
-        best_of(first, rank_col[:head], tail, rank_row[:, head:]),
-        best_of(tail, rank_col[head:], tail, rank_row[:, head:]),
-    )
-    for i, g in enumerate(order[:3]):
-        send_best[g] = best_first[:, part * i:part * (i + 1)]
-    send_best[last] = best_tail
-
-    @pl.loop(0, n)
-    def _(to):
-        @pl.when(to != me)
-        def _():
-            best_copy(to, me).start()
-
-    bests[me] = send_best[me // per]
+    def arrive(begin, end):
+        @pl.loop(begin, end)
+        def _(k):
+            @pl.when(k != home)
+            def _():
+                row_copy(other, k).wait_recv()
+
+    def send_back(begin, end):
+        @pl.loop(begin, end)
+        def _(to):
+            @pl.when(to != me)
+            def _():
+                best_copy(to, me).start()
+
+    def span(begin, end):
+        return rows[begin:end].reshape((end - begin) * cap, width)
+
+    early_row, late_row = rank_row[:, :3 * part], rank_row[:, 3 * part:]
+    early_col, late_col = rank_col[:3 * part], rank_col[3 * part:]
+    arrive(0, n - quarter)
+    best_early = best_of(span(0, n - quarter), early_col, span(0, n - quarter), early_row)
+    arrive(n - quarter, n)
+    fresh = span(n - quarter, n)
+    send_best[0] = jnp.maximum(
+        best_early[:, :part], best_of(fresh, late_col, span(0, quarter), early_row[:, :part])
+    )
+    send_back(0, quarter)
+    best_rest = jnp.maximum(
+        best_early[:, part:],
+        best_of(fresh, late_col, span(quarter, n - quarter), early_row[:, part:]),
+    )
+    best_late = jnp.maximum(
+        best_of(span(0, n - quarter), early_col, fresh, late_row),
+        best_of(fresh, late_col, fresh, late_row),
+    )
+    send_best[1] = best_rest[:, :part]
+    send_best[2] = best_rest[:, part:]
+    send_best[3] = best_late
+    send_back(quarter, n)
+    bests[me] = send_best[home // per]
+
+    keeper = lax.broadcasted_iota(jnp.int32, (n, 128), 0)
+    offset = jnp.zeros((n, 128), jnp.int32)
+    for c in range(n):
+        offset = jnp.where(keeper == c, place_of(me, c) % per * cap, offset)
 
     @pl.loop(0, n)
     def _(to):
@@ -322,10 +351,9 @@
         best_copy(at, at).wait()
 
     mine = jnp.concatenate([bests[c] for c in range(n)], axis=0)
-    place = (me % per) * cap + within
     for k in range(count // 128):
         piece = slice(128 * k, 128 * (k + 1))
-        at = jnp.broadcast_to(place[:, piece], (n, 128))
+        at = offset + within[:, piece]
         found = jnp.take_along_axis(mine, at, axis=1, mode="promise_in_bounds")
         out_ref[:, piece] = jnp.sum(
             jnp.where(named[:, piece] > 0.0, found, 0.0), axis=0, keepdims=True
@@ -365,7 +393,7 @@
         n = lax.axis_size("blk")
         slots = 2 * embeddings.shape[0]
         cap = slots // n
-        if n % 4 == 0 and slots == 512 and n // 4 * cap == 128:
+        if n == 16 and slots == 512 and cap == 32:
             return fused(embeddings, cluster, rank)
         return local(embeddings, cluster, rank)
 

time: 35 us -> 34.2 us (0.977)
  Pallas kernels: 34.3 us -> 33.4 us
    pallas_call x1, Pallas kernels: 34.3 us -> 33.4 us  [fused(): pl.pallas_call(functools.partial(kernel, n, cap), out_shape=pltpu.VMEM((1...]
where the time goes in v2:
time: 34.2 us; the launch traced here: 34 us
  Pallas kernels  33.4 us (98%)
  local copies, waits for them, and re-layouts  0.56 us (2%)
    pallas_call x1, Pallas kernels, fused(): pl.pallas_call(functools.partial(kernel, n, cap), out_shape=pltpu.VMEM((1...  33.4 us

profile of v2, /device:TPU:0, one launch (start us, length us, event | category | flops | bytes accessed | tf_op | source)
XLA Modules:
  0.0 34.0 jit_solution(11880882705471138315)
XLA Ops:
  0.0 33.4 %shard_map.37 = f32[1,256]{1,0:T(1,128)S(1)} custom-call(bf16[256,1024]{1,0:T(8,128)(2,1)} %emb_hbm.1, s32[1,256]{1,0:T(1,128)} %bitcast.4, s32[1,256]{1,0:T(1,128)} %bitcast.5), custom_call_target="tpu_custom_call" | custom-call | tf_op jit(solution)/shard_map/pallas_call | solution.py:369
  33.5 0.6 %copy.5 = f32[256]{0:T(256)} copy(f32[256]{0:T(256)S(1)} %bitcast.3) | data formatting | bytes 2048

commit v3 on v2

--- a/solution.py
+++ b/solution.py
@@ -72,7 +72,7 @@
     layer = me // quarter
     turn = me % quarter
     side = layer // 2
-    early = quarter - 1
+    early = quarter // 2
     middle = jnp.logical_or(layer == 1, layer == 2)
     near = 1 + layer % 2
     rim = 3 * side
@@ -109,6 +109,14 @@
         @pl.loop(1, quarter)
         def _(k):
             signal(barrier, own + lax.rem(turn + k, quarter))
+
+    @pl.when(jnp.logical_not(middle))
+    def _():
+        pl.semaphore_wait(barrier, quarter)
+
+        @pl.loop(0, quarter)
+        def _(k):
+            signal(edge_in, inward + k)
 
     loads[0].wait()
     target = cluster_ref[...]
@@ -193,14 +201,6 @@
     def _():
         pl.semaphore_wait(barrier, 2 * quarter - 1)
 
-    @pl.when(jnp.logical_not(middle))
-    def _():
-        pl.semaphore_wait(barrier, quarter)
-
-        @pl.loop(0, quarter)
-        def _(k):
-            signal(edge_in, inward + k)
-
     row_copy(lead).start()
     pack_send(inward, 1, 2)
     loads[1].wait()
@@ -231,14 +231,16 @@
     def _():
         pl.semaphore_wait(edge_in, quarter)
         signal(half_in, inward + turn)
-        pack_send(inward, 2, early)
         rank_all(rim * quarter, 0)
         rank_all(own, 1)
-        pack_send(rim * quarter, 0, quarter)
+        pack_send(inward, 2, early)
+        pack_all(far_rim * quarter, 0, 2)
         pl.semaphore_wait(half_in, 1)
         signal(all_in, rim * quarter + turn)
         rank_all(far_rim * quarter, 0)
-        pack_send(far_rim * quarter, 0, quarter)
+        send_all(far_rim * quarter, 0, 2)
+        pack_send(far_rim * quarter, 2, quarter)
+        pack_send(rim * quarter, 0, quarter)
         pack_send(inward, early, quarter)
         send_own()
 

time: 34.2 us -> 33.7 us (0.985)
  Pallas kernels: 33.4 us -> 33 us
    pallas_call x1, Pallas kernels: 33.4 us -> 33 us  [fused(): pl.pallas_call(functools.partial(kernel, n, cap), out_shape=pltpu.VMEM((1...]
where the time goes in v3:
time: 33.7 us; the launch traced here: 33.6 us
  Pallas kernels  33 us (98%)
  local copies, waits for them, and re-layouts  0.56 us (2%)
    pallas_call x1, Pallas kernels, fused(): pl.pallas_call(functools.partial(kernel, n, cap), out_shape=pltpu.VMEM((1...  33 us

profile of v3, /device:TPU:0, one launch (start us, length us, event | category | flops | bytes accessed | tf_op | source)
XLA Modules:
  0.0 33.6 jit_solution(1252554894139471669)
XLA Ops:
  0.0 33.0 %shard_map.37 = f32[1,256]{1,0:T(1,128)S(1)} custom-call(bf16[256,1024]{1,0:T(8,128)(2,1)} %emb_hbm.1, s32[1,256]{1,0:T(1,128)} %bitcast.4, s32[1,256]{1,0:T(1,128)} %bitcast.5), custom_call_target="tpu_custom_call" | custom-call | tf_op jit(solution)/shard_map/pallas_call | solution.py:371
  33.0 0.6 %copy.5 = f32[256]{0:T(256)} copy(f32[256]{0:T(256)S(1)} %bitcast.3) | data formatting | bytes 2048

commit v4 on v3

--- a/solution.py
+++ b/solution.py
@@ -176,8 +176,7 @@
         return lax.rem(turn // 2 + cross, 2) * 2 + lax.rem(turn + k // 2, 2)
 
     def pack_all(first, begin, end):
-        @pl.loop(begin, end)
-        def _(k):
+        for k in range(begin, end):
             pack(first + turned(k))
 
     def send_all(first, begin, end):
@@ -186,8 +185,7 @@
             row_copy(first + turned(k)).start()
 
     def pack_send(first, begin, end):
-        @pl.loop(begin, end)
-        def _(k):
+        for k in range(begin, end):
             to = first + turned(k)
             pack(to)
             row_copy(to).start()
@@ -219,8 +217,7 @@
             rank_copy(first + lax.rem(turn + k, quarter)).start()
 
     def send_own():
-        @pl.loop(1, quarter)
-        def _(k):
+        for k in range(1, quarter):
             to = own + lax.rem(turn + k, quarter)
             pack(to)
             row_copy(to).start()
@@ -303,8 +300,7 @@
                 row_copy(other, k).wait_recv()
 
     def send_back(begin, end):
-        @pl.loop(begin, end)
-        def _(to):
+        for to in range(begin, end):
             @pl.when(to != me)
             def _():
                 best_copy(to, me).start()
@@ -347,10 +343,22 @@
         def _():
             row_copy(to).wait_send()
 
+    def best_arrive(begin, end):
+        @pl.loop(begin, end)
+        def _(at):
+            @pl.when(at != me)
+            def _():
+                best_copy(at, at).wait_recv()
+
+    best_arrive(0, quarter)
+    best_arrive(3 * quarter, n)
+
     @pl.loop(1, n)
     def _(k):
         at = lax.rem(me + k, n)
-        best_copy(at, at).wait()
+        best_copy(at, at).wait_send()
+
+    best_arrive(quarter, 3 * quarter)
 
     mine = jnp.concatenate([bests[c] for c in range(n)], axis=0)
     for k in range(count // 128):

time: 33.7 us -> 33.7 us (level)
  no operation moved by 1% of the time
where the time goes in v4:
time: 33.7 us; the launch traced here: 33.5 us
  Pallas kernels  33 us (98%)
  local copies, waits for them, and re-layouts  0.56 us (2%)
    pallas_call x1, Pallas kernels, fused(): pl.pallas_call(functools.partial(kernel, n, cap), out_shape=pltpu.VMEM((1...  33 us

profile of v4, /device:TPU:0, one launch (start us, length us, event | category | flops | bytes accessed | tf_op | source)
XLA Modules:
  0.0 33.5 jit_solution(3847424103270412464)
XLA Ops:
  0.0 33.0 %shard_map.37 = f32[1,256]{1,0:T(1,128)S(1)} custom-call(bf16[256,1024]{1,0:T(8,128)(2,1)} %emb_hbm.1, s32[1,256]{1,0:T(1,128)} %bitcast.4, s32[1,256]{1,0:T(1,128)} %bitcast.5), custom_call_target="tpu_custom_call" | custom-call | tf_op jit(solution)/shard_map/pallas_call | solution.py:379
  33.0 0.6 %copy.5 = f32[256]{0:T(256)} copy(f32[256]{0:T(256)S(1)} %bitcast.3) | data formatting | bytes 2048
